TPU v7x, 128 devices: a whole 4x4x4 slice. The times are simulated.
128 devices in a mesh: dp: 8 (over z, core), mp: 16 (over y, x).
Axes of the slice: x: 4, y: 4, z: 4, core: 2. Of those that a mesh axis runs over, the one named last changes fastest.
Arguments:
- crop_hidden: bfloat16 [8, 1536, 8192], P(None, 'dp', 'mp'), may hold values from -15 to 15
- projector_weight: bfloat16 [8192, 8192], P('mp'), may hold values from -0.21213203 to 0.21213203
- pairing: int32 [8, 1536], P(None, 'dp'), may hold values from 0 to 191, as said below
Outputs:
- embeddings: float32 [8192, 8, 1536], P('mp', 'dp')
- loss_terms: float32 [4], replicated
Inputs may be any that keep to these rules, and one draw needn't show every extreme that they name: Each aligned block of 192 entries of a row of pairing is a permutation of 0 to 191.
All inputs are finite; a program needn't handle non-finite values.
Results may differ from a plain program's by a relative error of at most 0.0003.
Values may be sent and summed in bfloat16 or wider, within the bound.
No kernel may reach another device: no remote copies, remote signals or barrier semaphores. Data moves between devices by JAX's collectives and lax.ppermute only.
A program may use at most 128 MiB of HBM per device.

v0:
```python
import functools
import jax
import jax.numpy as jnp
from jax import lax
from jax.sharding import Mesh
from jax.sharding import PartitionSpec as P

MP = ("mp_0", "mp_1")
DP = ("dp_0", "dp_1")
DP_MP = ("dp_0", "dp_1", "mp_0", "mp_1")
highest = lax.Precision.HIGHEST
epsilon = 0.0001


def by_axis(x, axes):
    return functools.reduce(lax.psum, axes, x)


def local(crop_hidden, projector_weight, pairing):
    crop_count, local_rows, width_part = crop_hidden.shape
    features = projector_weight.shape[1]
    total_rows = crop_count * local_rows
    column_block = lax.all_to_all(projector_weight, MP, split_axis=1, concat_axis=0, tiled=True)
    shards = lax.all_gather(crop_hidden, MP, axis=2, tiled=True)
    flat_piece = shards.reshape(total_rows, shards.shape[2])
    embedded = lax.dot_general(
        column_block, flat_piece, (((0,), (1,)), ((), ())), preferred_element_type=jnp.float32
    )
    feature_part = embedded.shape[0]
    by_crop = embedded.reshape(feature_part, crop_count, local_rows)
    onehot = (pairing[:, :, None] == jnp.arange(local_rows, dtype=jnp.int32)[None, None, :]).astype(
        jnp.float32
    )
    aligned = jnp.einsum("jcr,cri->jci", by_crop, onehot, precision=highest)
    invariance = 0.0
    for anchor in range(2):
        differ = aligned - aligned[:, anchor : anchor + 1, :]
        invariance = invariance + jnp.sum(differ * differ)
    owned_block = lax.all_to_all(by_crop, DP, split_axis=1, concat_axis=2, tiled=True)
    batch_rows = owned_block.shape[2]
    column_mean = jnp.mean(owned_block, axis=2, keepdims=True)
    centered = owned_block - column_mean
    variance = jnp.sum(centered * centered, axis=2) / (batch_rows - 1)
    hinge_sum = jnp.sum(jax.nn.relu(1.0 - jnp.sqrt(variance + epsilon)))
    diagonal_sq = jnp.sum(variance * variance)
    gram_scale = 1.0 / ((batch_rows - 1) * (batch_rows - 1))
    partial_gram = jnp.einsum("jcr,jcs->crs", centered, centered, precision=highest)
    gram_block = lax.psum(partial_gram.astype(jnp.bfloat16), MP).astype(jnp.float32)
    frobenius = jnp.where(
        lax.axis_index(MP) == 0, jnp.sum(gram_block * gram_block) * gram_scale, 0.0
    )
    totals = (
        by_axis(invariance, DP_MP),
        by_axis(hinge_sum, DP_MP),
        by_axis(frobenius - diagonal_sq, DP_MP),
    )
    invariance_loss = totals[0] / (2 * (crop_count - 1) * batch_rows * features)
    variance_loss = totals[1] / (crop_count * features)
    covariance_loss = totals[2] / (crop_count * features)
    total_loss = 25.0 * invariance_loss + 25.0 * variance_loss + covariance_loss
    loss_terms = jnp.stack([invariance_loss, variance_loss, covariance_loss, total_loss])
    return (owned_block, loss_terms)


def solution(mesh):
    torus = Mesh(mesh.devices.reshape(4, 2, 4, 4), ("dp_0", "dp_1", "mp_0", "mp_1"))
    placed = (P(None, DP, MP), P(MP, None), P(None, DP))
    return jax.shard_map(
        local, mesh=torus, in_specs=placed, out_specs=(P(MP, DP, None), P()), check_vma=False
    )
```

profile of v0, /device:TPU:0, one launch (start us, length us, event | category | flops | bytes accessed | tf_op | source)
XLA Modules:
  0.0 498.9 jit_solution(17605152332946094416)
XLA Ops:
  7.2 0.0 all-gather.2.cloned.1.call-start
  7.2 0.7 all-gather.2.cloned.1.call-update
  7.9 0.0 all-reduce.6.cloned.1.call-start
  7.9 7.5 %copy.9 = bf16[64,16,8,512]{3,2,0,1:T(8,128)(2,1)} copy(bf16[64,16,8,512]{3,2,1,0:T(8,128)(2,1)} %bitcast.30) | data formatting | bytes 16777216 | tf_op jit(solution)/shard_map/all_to_all | solution.py:23
  15.4 128.3 %all_to_all.31 = bf16[512,16,512]{2,0,1:T(8,128)(2,1)} all-to-all(bf16[512,16,512]{2,0,1:T(8,128)(2,1)} %bitcast.29), channel_id=1, replica_groups=mesh['dp_0'=4,'dp_1'=2,'mp_0'=4,'mp_1'=4] {'mp_0','mp_1'}, dimensions={1} | all-to-all | bytes 16777216 | tf_op jit(solution)/shard_map/all_to_all | solution.py:23
  143.8 117.0 %all-gather.2.cloned.1.call-done = bf16[8,192,8192]{2,1,0:T(8,128)(2,1)} async-done(((bf16[8,192,512]{2,1,0:T(8,128)(2,1)}), bf16[8,192,8192]{2,1,0:T(8,128)(2,1)}) %all-gather.2.cloned.1.call-update) | async-done | bytes 25165840 | tf_op jit(solution)/shard_map/all_gather | solution.py:24
  260.8 18.9 %fusion.2 = f32[512,8,192]{0,2,1:T(8,128)S(1)} fusion(bf16[8192,512,1]{1,0,2:T(8,128)(2,1)} %bitcast.31, bf16[8,192,8192]{2,1,0:T(8,128)(2,1)} %all-gather.2.cloned.1.call-done), kind=kOutput, calls=%fused_computation.17 | convolution fusion | flops 12884901888 | bytes 36700160 | tf_op jit(solution)/shard_map/dot_general | solution.py:26
  279.7 0.0 copy-start
  279.7 1.7 copy-done
  281.3 42.7 %all_to_all.32 = f32[512,8,192]{0,2,1:T(8,128)S(1)} all-to-all(f32[512,8,192]{0,2,1:T(8,128)S(1)} %fusion.2), channel_id=1, replica_groups=mesh['dp_0'=4,'dp_1'=2,'mp_0'=4,'mp_1'=4] {'dp_0','dp_1'}, dimensions={1} | all-to-all | bytes 6291456 | tf_op jit(solution)/shard_map/all_to_all | solution.py:39
  324.0 0.3 reduce_sum.65
  324.3 0.6 multiply_reduce_fusion.1
  324.8 16.8 %fusion = bf16[1,1536,1536]{2,1,0:T(8,128)(2,1)} fusion(f32[512,1536]{0,1:T(8,128)S(1)} %bitcast.32), kind=kOutput, calls=%fused_computation.3 | convolution fusion | flops 14497873920 | bytes 7864320 | tf_op jit(solution)/shard_map/jcr,jcs->crs/dot_general | solution.py:47
  341.6 0.0 copy-start.1
  341.6 0.0 all-reduce.6.cloned.1.call-update
  341.6 0.7 copy-done.1
  342.3 3.9 convolution_bitcast_fusion
  346.2 0.1 slice_bitcast_fusion.1
  346.2 2.0 multiply_reduce_fusion.2
  349.5 5.4 %copy.6 = f32[512,1,1536]{2,1,0:T(1,128)} copy(f32[512,1,1536]{0,2,1:T(8,128)S(1)} %bitcast.28) | data formatting | bytes 6291456
  354.9 0.7 multiply_reduce_fusion.4
  355.6 91.4 %all-reduce.6.cloned.1.call-done = bf16[1,1536,1536]{2,1,0:T(8,128)(2,1)} async-done(((bf16[1,1536,1536]{2,1,0:T(8,128)(2,1)}), bf16[1,1536,1536]{2,1,0:T(8,128)(2,1)}) %all-reduce.6.cloned.1.call-update) | async-done | bytes 4718608 | tf_op jit(solution)/shard_map/psum | solution.py:48
  447.0 5.3 %multiply_reduce_fusion = f32[]{:T(128)} fusion(bf16[1,1536,1536]{2,1,0:T(8,128)(2,1)} %all-reduce.6.cloned.1.call-done), kind=kLoop, calls=%fused_computation | loop fusion | flops 7077887 | bytes 4718596 | tf_op jit(solution)/shard_map/reduce_sum | solution.py:50
  453.5 11.3 %all-reduce.2 = (f32[]{:T(128)}, f32[]{:T(128)}, f32[]{:T(128)}) all-reduce(f32[]{:T(128)S(6)} %add.47, f32[]{:T(128)} %get-tuple-element.7, f32[]{:T(128)S(6)} %sub.61), channel_id=1, replica_groups=mesh['dp_0'=4,'dp_1'=2,'mp_0'=4,'mp_1'=4] {'dp_0'}, use_global_device_ids=true, to_apply=%region_2.0 | all-reduce | flops 3 | bytes 24 | tf_op jit(solution)/shard_map/psum | solution.py:16
  464.8 3.2 all-reduce.3
  467.9 11.0 %all-reduce.1 = (f32[]{:T(128)}, f32[]{:T(128)}, f32[]{:T(128)}) all-reduce(f32[]{:T(128)} %get-tuple-element.17, f32[]{:T(128)} %get-tuple-element.18, f32[]{:T(128)} %get-tuple-element.19), channel_id=1, replica_groups=mesh['dp_0'=4,'dp_1'=2,'mp_0'=4,'mp_1'=4] {'mp_0'}, use_global_device_ids=true, to_apply=%region_4.5 | all-reduce | flops 3 | bytes 24 | tf_op jit(solution)/shard_map/psum | solution.py:16
  478.9 9.4 %all-reduce = (f32[]{:T(128)}, f32[]{:T(128)}, f32[]{:T(128)}) all-reduce(f32[]{:T(128)} %get-tuple-element.11, f32[]{:T(128)} %get-tuple-element.12, f32[]{:T(128)} %get-tuple-element.13), channel_id=1, replica_groups=mesh['dp_0'=4,'dp_1'=2,'mp_0'=4,'mp_1'=4] {'mp_1'}, use_global_device_ids=true, to_apply=%region_5.6 | all-reduce | flops 3 | bytes 24 | tf_op jit(solution)/shard_map/psum | solution.py:16
  491.5 0.6 pad_maximum_fusion
  (1 shorter events, 0.0 us)
Async XLA Ops:
  7.2 253.6 %all-gather.2.cloned.1.call-start = ((), (), s32[]{:S(2)}) async-start(), calls=%async_computation.2 | async-start | bytes 26738688 | tf_op jit(solution)/shard_map/all_gather | solution.py:24
  7.9 439.1 %all-reduce.6.cloned.1.call-start = ((), (), s32[]{:S(2)}) async-start(), calls=%async_computation.3 | async-start | bytes 9437184 | tf_op jit(solution)/shard_map/psum | solution.py:48
  279.7 1.7 copy-start
  341.6 0.7 copy-start.1
Sparse Core Ops, SparseCore 0:
  10.1 250.6 all-gather.1
  341.7 105.2 all-reduce.5
where the time goes:
time: 499 us
  waiting for transfers between devices  209 us (42%)
  blocking collectives  206 us (41%)
  matrix products  39.5 us (8%)
  between operations  19.8 us (4%)
  local copies, waits for them, and re-layouts  15.3 us (3%)
  other arithmetic  9.4 us (2%)
    all_to_all x1, blocking collectives, local(): lax.all_to_all(projector_weight, MP, split_axis=1, concat_axis=0, tiled=T...  128 us
    all_gather x1, waiting for transfers between devices, local(): shards = lax.all_gather(crop_hidden, MP, axis=2, tiled=True)  117 us
    psum x1, waiting for transfers between devices, local(): lax.psum(partial_gram.astype(jnp.bfloat16), MP).astype(jnp.float32)  91.4 us
    all_to_all x1, blocking collectives, local(): lax.all_to_all(by_crop, DP, split_axis=1, concat_axis=2, tiled=True)  42.7 us
    psum x4, blocking collectives, by_axis(): return functools.reduce(lax.psum, axes, x)  34.8 us
    dot_general x1, matrix products, local(): lax.dot_general(column_block, flat_piece, (((0,), (1,)), ((), ())), prefe...  18.9 us
    dot_general x1, matrix products, local(): jnp.einsum('jcr,jcs->crs', centered, centered, precision=highest)  16.8 us
  transfers between devices with their start and end apart: 2, of which 2 were waited for; matrix products, arithmetic and copies ran while one was open for 4% of the time, Pallas kernels for 0%

commit v1 on v0

--- a/solution.py
+++ b/solution.py
@@ -10,6 +10,11 @@
 DP_MP = ("dp_0", "dp_1", "mp_0", "mp_1")
 highest = lax.Precision.HIGHEST
 epsilon = 0.0001
+
+
+def axis_by_axis(array, first, second):
+    partial = lax.psum(array, first)
+    return lax.psum(partial, second)
 
 
 def by_axis(x, axes):
@@ -45,7 +50,7 @@
     diagonal_sq = jnp.sum(variance * variance)
     gram_scale = 1.0 / ((batch_rows - 1) * (batch_rows - 1))
     partial_gram = jnp.einsum("jcr,jcs->crs", centered, centered, precision=highest)
-    gram_block = lax.psum(partial_gram.astype(jnp.bfloat16), MP).astype(jnp.float32)
+    gram_block = axis_by_axis(partial_gram.astype(jnp.bfloat16), "mp_1", "mp_0").astype(jnp.float32)
     frobenius = jnp.where(
         lax.axis_index(MP) == 0, jnp.sum(gram_block * gram_block) * gram_scale, 0.0
     )

time: 499 us -> 596 us (1.19)
  waiting for transfers between devices: 209 us -> 307 us
    psum x1 -> x2, waiting for transfers between devices: 91.4 us -> 189 us  [the longest x1 98.6 us: axis_by_axis(): partial = lax.psum(array, first)]
  transfers between devices with their start and end apart: 2 -> 3, of which waited for: 2 -> 3; matrix products, arithmetic and copies ran while one was open for 4% -> 3% of each run, Pallas kernels for 0% -> 0%
where the time goes in v1:
time: 596 us
  waiting for transfers between devices  307 us (52%)
  blocking collectives  206 us (35%)
  matrix products  39.5 us (7%)
  between operations  19.7 us (3%)
  local copies, waits for them, and re-layouts  14.6 us (2%)
  other arithmetic  9.51 us (2%)
    all_to_all x1, blocking collectives, local(): lax.all_to_all(projector_weight, MP, split_axis=1, concat_axis=0, tiled=T...  128 us
    all_gather x1, waiting for transfers between devices, local(): shards = lax.all_gather(crop_hidden, MP, axis=2, tiled=True)  117 us
    psum x1, waiting for transfers between devices, axis_by_axis(): partial = lax.psum(array, first)  98.6 us
    psum x1, waiting for transfers between devices, axis_by_axis(): return lax.psum(partial, second)  90.2 us
    all_to_all x1, blocking collectives, local(): lax.all_to_all(by_crop, DP, split_axis=1, concat_axis=2, tiled=True)  42.7 us
    psum x4, blocking collectives, by_axis(): return functools.reduce(lax.psum, axes, x)  34.8 us
    dot_general x1, matrix products, local(): lax.dot_general(column_block, flat_piece, (((0,), (1,)), ((), ())), prefe...  18.9 us
    dot_general x1, matrix products, local(): jnp.einsum('jcr,jcs->crs', centered, centered, precision=highest)  16.8 us
  transfers between devices with their start and end apart: 3, of which 3 were waited for; matrix products, arithmetic and copies ran while one was open for 3% of the time, Pallas kernels for 0%

profile of v1, /device:TPU:0, one launch (start us, length us, event | category | flops | bytes accessed | tf_op | source)
XLA Modules:
  0.0 595.9 jit_solution(983775859717368523)
XLA Ops:
  7.2 0.0 all-gather.2.cloned.1.call-start
  7.2 0.7 all-gather.2.cloned.1.call-update
  7.9 0.0 all-reduce.7.cloned.1.call-start
  7.9 7.5 %copy.9 = bf16[64,16,8,512]{3,2,0,1:T(8,128)(2,1)} copy(bf16[64,16,8,512]{3,2,1,0:T(8,128)(2,1)} %bitcast.30) | data formatting | bytes 16777216 | tf_op jit(solution)/shard_map/all_to_all | solution.py:28
  15.4 128.3 %all_to_all.31 = bf16[512,16,512]{2,0,1:T(8,128)(2,1)} all-to-all(bf16[512,16,512]{2,0,1:T(8,128)(2,1)} %bitcast.29), channel_id=1, replica_groups=mesh['dp_0'=4,'dp_1'=2,'mp_0'=4,'mp_1'=4] {'mp_0','mp_1'}, dimensions={1} | all-to-all | bytes 16777216 | tf_op jit(solution)/shard_map/all_to_all | solution.py:28
  143.8 117.0 %all-gather.2.cloned.1.call-done = bf16[8,192,8192]{2,1,0:T(8,128)(2,1)} async-done(((bf16[8,192,512]{2,1,0:T(8,128)(2,1)}), bf16[8,192,8192]{2,1,0:T(8,128)(2,1)}) %all-gather.2.cloned.1.call-update) | async-done | bytes 25165840 | tf_op jit(solution)/shard_map/all_gather | solution.py:29
  260.8 18.9 %fusion.2 = f32[512,8,192]{0,2,1:T(8,128)S(1)} fusion(bf16[8192,512,1]{1,0,2:T(8,128)(2,1)} %bitcast.31, bf16[8,192,8192]{2,1,0:T(8,128)(2,1)} %all-gather.2.cloned.1.call-done), kind=kOutput, calls=%fused_computation.17 | convolution fusion | flops 12884901888 | bytes 36700160 | tf_op jit(solution)/shard_map/dot_general | solution.py:31
  279.7 0.0 copy-start
  279.7 1.7 copy-done
  281.3 42.7 %all_to_all.32 = f32[512,8,192]{0,2,1:T(8,128)S(1)} all-to-all(f32[512,8,192]{0,2,1:T(8,128)S(1)} %fusion.2), channel_id=1, replica_groups=mesh['dp_0'=4,'dp_1'=2,'mp_0'=4,'mp_1'=4] {'dp_0','dp_1'}, dimensions={1} | all-to-all | bytes 6291456 | tf_op jit(solution)/shard_map/all_to_all | solution.py:44
  324.0 0.3 reduce_sum.65
  324.3 0.6 multiply_reduce_fusion.1
  324.8 16.8 %fusion = bf16[1,1536,1536]{2,1,0:T(8,128)(2,1)} fusion(f32[512,1536]{0,1:T(8,128)S(1)} %bitcast.32), kind=kOutput, calls=%fused_computation.3 | convolution fusion | flops 14497873920 | bytes 7864320 | tf_op jit(solution)/shard_map/jcr,jcs->crs/dot_general | solution.py:52
  341.6 0.0 all-reduce.7.cloned.1.call-update
  341.6 0.0 copy-start.1
  341.6 0.2 all-reduce.9.cloned.1.call-start
  341.8 98.6 %all-reduce.7.cloned.1.call-done = bf16[1,1536,1536]{2,1,0:T(8,128)(2,1)} async-done(((bf16[1,1536,1536]{2,1,0:T(8,128)(2,1)}), bf16[1,1536,1536]{2,1,0:T(8,128)(2,1)}) %all-reduce.7.cloned.1.call-update) | async-done | bytes 4718608 | tf_op jit(solution)/shard_map/psum | solution.py:16
  440.4 0.0 all-reduce.9.cloned.1.call-update
  440.4 0.0 copy-done.1
  440.4 3.9 convolution_bitcast_fusion
  444.3 0.1 slice_bitcast_fusion.1
  444.4 2.0 multiply_reduce_fusion.2
  447.7 5.4 copy.6
  453.1 0.7 multiply_reduce_fusion.4
  453.8 90.2 %all-reduce.9.cloned.1.call-done = bf16[1,1536,1536]{2,1,0:T(8,128)(2,1)} async-done(((bf16[1,1536,1536]{2,1,0:T(8,128)(2,1)}), bf16[1,1536,1536]{2,1,0:T(8,128)(2,1)}) %all-reduce.9.cloned.1.call-update) | async-done | bytes 4718608 | tf_op jit(solution)/shard_map/psum | solution.py:17
  544.0 5.4 multiply_reduce_fusion
  550.8 11.3 %all-reduce.2 = (f32[]{:T(128)}, f32[]{:T(128)}, f32[]{:T(128)}) all-reduce(f32[]{:T(128)S(6)} %add.49, f32[]{:T(128)} %get-tuple-element.7, f32[]{:T(128)S(6)} %sub.61), channel_id=1, replica_groups=mesh['dp_0'=4,'dp_1'=2,'mp_0'=4,'mp_1'=4] {'dp_0'}, use_global_device_ids=true, to_apply=%region_2.0 | all-reduce | flops 3 | bytes 24 | tf_op jit(solution)/shard_map/psum | solution.py:21
  562.0 3.2 all-reduce.3
  565.2 9.2 %all-reduce.1 = (f32[]{:T(128)}, f32[]{:T(128)}, f32[]{:T(128)}) all-reduce(f32[]{:T(128)} %get-tuple-element.17, f32[]{:T(128)} %get-tuple-element.18, f32[]{:T(128)} %get-tuple-element.19), channel_id=1, replica_groups=mesh['dp_0'=4,'dp_1'=2,'mp_0'=4,'mp_1'=4] {'mp_0'}, use_global_device_ids=true, to_apply=%region_4.5 | all-reduce | flops 3 | bytes 24 | tf_op jit(solution)/shard_map/psum | solution.py:21
  574.5 11.1 %all-reduce = (f32[]{:T(128)}, f32[]{:T(128)}, f32[]{:T(128)}) all-reduce(f32[]{:T(128)} %get-tuple-element.11, f32[]{:T(128)} %get-tuple-element.12, f32[]{:T(128)} %get-tuple-element.13), channel_id=1, replica_groups=mesh['dp_0'=4,'dp_1'=2,'mp_0'=4,'mp_1'=4] {'mp_1'}, use_global_device_ids=true, to_apply=%region_5.6 | all-reduce | flops 3 | bytes 24 | tf_op jit(solution)/shard_map/psum | solution.py:21
  588.8 0.6 pad_maximum_fusion
  (1 shorter events, 0.0 us)
Async XLA Ops:
  7.2 253.6 %all-gather.2.cloned.1.call-start = ((), (), s32[]{:S(2)}) async-start(), calls=%async_computation.2 | async-start | bytes 26738688 | tf_op jit(solution)/shard_map/all_gather | solution.py:29
  7.9 432.5 %all-reduce.7.cloned.1.call-start = ((), (), s32[]{:S(2)}) async-start(), calls=%async_computation.3 | async-start | bytes 9437184 | tf_op jit(solution)/shard_map/psum | solution.py:16
  279.7 1.7 copy-start
  341.6 98.8 %copy-start.1 = (s32[8,192]{1,0:T(8,128)S(1)}, s32[8,192]{1,0:T(8,128)}, u32[]{:S(2)}) copy-start(s32[8,192]{1,0:T(8,128)} %param.5) | copy-start | bytes 18436
  341.6 202.4 %all-reduce.9.cloned.1.call-start = ((), (), s32[]{:S(2)}) async-start(), calls=%async_computation.4 | async-start | bytes 9437184 | tf_op jit(solution)/shard_map/psum | solution.py:17
Sparse Core Ops, SparseCore 0:
  10.1 250.6 all-gather.1
  341.7 98.6 all-reduce.6
  442.8 101.1 all-reduce.8

commit v2 on v0

--- a/solution.py
+++ b/solution.py
@@ -21,7 +21,8 @@
     features = projector_weight.shape[1]
     total_rows = crop_count * local_rows
     column_block = lax.all_to_all(projector_weight, MP, split_axis=1, concat_axis=0, tiled=True)
-    shards = lax.all_gather(crop_hidden, MP, axis=2, tiled=True)
+    blocks = lax.all_gather(crop_hidden, MP, axis=0, tiled=False)
+    shards = jnp.concatenate(blocks, axis=2)
     flat_piece = shards.reshape(total_rows, shards.shape[2])
     embedded = lax.dot_general(
         column_block, flat_piece, (((0,), (1,)), ((), ())), preferred_element_type=jnp.float32

time: 499 us -> 486 us (0.974)
  local copies, waits for them, and re-layouts: 15.3 us -> 32.2 us
  waiting for transfers between devices: 209 us -> 193 us
  blocking collectives: 206 us -> 191 us
    all_gather x1, waiting for transfers between devices: 117 us -> 101 us  [local(): blocks = lax.all_gather(crop_hidden, MP, axis=0, tiled=False)]
    all_to_all x1, blocking collectives: 128 us -> 114 us  [local(): lax.all_to_all(projector_weight, MP, split_axis=1, concat_axis=0, tiled=T...]
    unnamed x5 -> x6, local copies, waits for them, and re-layouts: 7.75 us -> 19.7 us
  transfers between devices with their start and end apart: 2 -> 2, of which waited for: 2 -> 2; matrix products, arithmetic and copies ran while one was open for 4% -> 8% of each run, Pallas kernels for 0% -> 0%
where the time goes in v2:
time: 486 us; the launch traced here: 485 us
  waiting for transfers between devices  193 us (40%)
  blocking collectives  191 us (39%)
  matrix products  39.5 us (8%)
  local copies, waits for them, and re-layouts  32.2 us (7%)
  between operations  19.8 us (4%)
  other arithmetic  9.4 us (2%)
    all_to_all x1, blocking collectives, local(): lax.all_to_all(projector_weight, MP, split_axis=1, concat_axis=0, tiled=T...  114 us
    all_gather x1, waiting for transfers between devices, local(): blocks = lax.all_gather(crop_hidden, MP, axis=0, tiled=False)  101 us
    psum x1, waiting for transfers between devices, local(): lax.psum(partial_gram.astype(jnp.bfloat16), MP).astype(jnp.float32)  91.3 us
    all_to_all x1, blocking collectives, local(): lax.all_to_all(by_crop, DP, split_axis=1, concat_axis=2, tiled=True)  42.6 us
    psum x4, blocking collectives, by_axis(): return functools.reduce(lax.psum, axes, x)  34.8 us
    unnamed x6, local copies, waits for them, and re-layouts  19.7 us
    dot_general x1, matrix products, local(): lax.dot_general(column_block, flat_piece, (((0,), (1,)), ((), ())), prefe...  18.9 us
    dot_general x1, matrix products, local(): jnp.einsum('jcr,jcs->crs', centered, centered, precision=highest)  16.8 us
  transfers between devices with their start and end apart: 2, of which 2 were waited for; matrix products, arithmetic and copies ran while one was open for 8% of the time, Pallas kernels for 0%

profile of v2, /device:TPU:0, one launch (start us, length us, event | category | flops | bytes accessed | tf_op | source)
XLA Modules:
  0.0 485.4 jit_solution(14091650747524074656)
XLA Ops:
  7.2 0.0 all-gather.3.cloned.1.call-start
  7.2 0.7 all-gather.3.cloned.1.call-update
  7.9 0.0 all-reduce.6.cloned.1.call-start
  7.9 12.0 %copy.10 = bf16[512,8192]{0,1:T(8,128)(2,1)} copy(bf16[512,8192]{1,0:T(8,128)(2,1)} %param.4) | data formatting | bytes 16777216 | tf_op args[1]
  19.9 12.4 %copy.11 = bf16[512,16,512]{2,0,1:T(8,128)(2,1)} copy(bf16[512,16,512]{0,2,1:T(8,128)(2,1)} %bitcast.36) | data formatting | bytes 16777216 | tf_op jit(solution)/shard_map/all_to_all | solution.py:23
  32.3 113.6 %all_to_all.28 = bf16[512,16,512]{2,0,1:T(8,128)(2,1)} all-to-all(bf16[512,16,512]{2,0,1:T(8,128)(2,1)} %copy.11), channel_id=1, replica_groups=mesh['dp_0'=4,'dp_1'=2,'mp_0'=4,'mp_1'=4] {'mp_0','mp_1'}, dimensions={1} | all-to-all | bytes 16777216 | tf_op jit(solution)/shard_map/all_to_all | solution.py:23
  145.9 101.4 %all-gather.3.cloned.1.call-done = bf16[128,192,512]{2,1,0:T(8,128)(2,1)} async-done(((bf16[8,192,512]{2,1,0:T(8,128)(2,1)}), bf16[128,192,512]{2,1,0:T(8,128)(2,1)}) %all-gather.3.cloned.1.call-update) | async-done | bytes 25165840 | tf_op jit(solution)/shard_map/all_gather | solution.py:24
  247.3 18.9 %fusion.5 = f32[512,8,192]{0,2,1:T(8,128)S(1)} fusion(bf16[16,8,192,512]{3,2,1,0:T(8,128)(2,1)} %bitcast.38, bf16[512,16,512]{2,0,1:T(8,128)(2,1)} %all_to_all.28), kind=kOutput, calls=%fused_computation.10 | convolution fusion | flops 12884901888 | bytes 36700160 | tf_op jit(solution)/shard_map/dot_general | solution.py:27
  266.2 0.0 copy-start
  266.2 1.7 copy-done
  267.9 42.6 %all_to_all.29 = f32[512,8,192]{0,2,1:T(8,128)S(1)} all-to-all(f32[512,8,192]{0,2,1:T(8,128)S(1)} %fusion.5), channel_id=1, replica_groups=mesh['dp_0'=4,'dp_1'=2,'mp_0'=4,'mp_1'=4] {'dp_0','dp_1'}, dimensions={1} | all-to-all | bytes 6291456 | tf_op jit(solution)/shard_map/all_to_all | solution.py:40
  310.5 0.3 reduce_sum.65
  310.8 0.6 multiply_reduce_fusion.1
  311.3 16.8 %fusion.4 = bf16[1,1536,1536]{2,1,0:T(8,128)(2,1)} fusion(f32[512,1536]{0,1:T(8,128)S(1)} %bitcast.37), kind=kOutput, calls=%fused_computation.6 | convolution fusion | flops 14497873920 | bytes 7864320 | tf_op jit(solution)/shard_map/jcr,jcs->crs/dot_general | solution.py:48
  328.1 0.0 copy-start.1
  328.1 0.0 all-reduce.6.cloned.1.call-update
  328.1 0.7 copy-done.1
  328.8 3.9 convolution_bitcast_fusion
  332.7 0.1 slice_bitcast_fusion.1
  332.7 2.0 multiply_reduce_fusion.2
  336.0 5.4 %copy.13 = f32[512,1,1536]{2,1,0:T(1,128)} copy(f32[512,1,1536]{0,2,1:T(8,128)S(1)} %bitcast.35) | data formatting | bytes 6291456
  341.5 0.7 multiply_reduce_fusion.4
  342.1 91.3 %all-reduce.6.cloned.1.call-done = bf16[1,1536,1536]{2,1,0:T(8,128)(2,1)} async-done(((bf16[1,1536,1536]{2,1,0:T(8,128)(2,1)}), bf16[1,1536,1536]{2,1,0:T(8,128)(2,1)}) %all-reduce.6.cloned.1.call-update) | async-done | bytes 4718608 | tf_op jit(solution)/shard_map/psum | solution.py:49
  433.5 5.3 %multiply_reduce_fusion = f32[]{:T(128)} fusion(bf16[1,1536,1536]{2,1,0:T(8,128)(2,1)} %all-reduce.6.cloned.1.call-done), kind=kLoop, calls=%fused_computation.3 | loop fusion | flops 7077887 | bytes 4718596 | tf_op jit(solution)/shard_map/reduce_sum | solution.py:51
  440.0 11.3 %all-reduce.2 = (f32[]{:T(128)}, f32[]{:T(128)}, f32[]{:T(128)}) all-reduce(f32[]{:T(128)S(6)} %add.47, f32[]{:T(128)} %get-tuple-element.11, f32[]{:T(128)S(6)} %sub.61), channel_id=1, replica_groups=mesh['dp_0'=4,'dp_1'=2,'mp_0'=4,'mp_1'=4] {'dp_0'}, use_global_device_ids=true, to_apply=%region_2.0 | all-reduce | flops 3 | bytes 24 | tf_op jit(solution)/shard_map/psum | solution.py:16
  451.3 3.2 all-reduce.3
  454.4 11.0 %all-reduce.1 = (f32[]{:T(128)}, f32[]{:T(128)}, f32[]{:T(128)}) all-reduce(f32[]{:T(128)} %get-tuple-element.21, f32[]{:T(128)} %get-tuple-element.22, f32[]{:T(128)} %get-tuple-element.23), channel_id=1, replica_groups=mesh['dp_0'=4,'dp_1'=2,'mp_0'=4,'mp_1'=4] {'mp_0'}, use_global_device_ids=true, to_apply=%region_4.5 | all-reduce | flops 3 | bytes 24 | tf_op jit(solution)/shard_map/psum | solution.py:16
  465.4 9.4 %all-reduce = (f32[]{:T(128)}, f32[]{:T(128)}, f32[]{:T(128)}) all-reduce(f32[]{:T(128)} %get-tuple-element.15, f32[]{:T(128)} %get-tuple-element.16, f32[]{:T(128)} %get-tuple-element.17), channel_id=1, replica_groups=mesh['dp_0'=4,'dp_1'=2,'mp_0'=4,'mp_1'=4] {'mp_1'}, use_global_device_ids=true, to_apply=%region_5.6 | all-reduce | flops 3 | bytes 24 | tf_op jit(solution)/shard_map/psum | solution.py:16
  478.0 0.6 pad_maximum_fusion
  (1 shorter events, 0.0 us)
Async XLA Ops:
  7.2 240.2 %all-gather.3.cloned.1.call-start = ((), (), s32[]{:S(2)}) async-start(), calls=%async_computation.3 | async-start | bytes 26738688 | tf_op jit(solution)/shard_map/all_gather | solution.py:24
  7.9 425.6 %all-reduce.6.cloned.1.call-start = ((), (), s32[]{:S(2)}) async-start(), calls=%async_computation.2 | async-start | bytes 9437184 | tf_op jit(solution)/shard_map/psum | solution.py:49
  266.2 1.7 copy-start
  328.1 0.7 copy-start.1
Sparse Core Ops, SparseCore 0:
  10.1 237.1 all-gather.2
  328.2 105.1 all-reduce.5
